TPU v7x, 32 devices: a whole 2x2x4 slice. The times are simulated.
32 devices in a mesh: rows: 4 (over x, core), cols: 8 (over z, y).
Axes of the slice: x: 2, y: 2, z: 4, core: 2. Of those that a mesh axis runs over, the one named last changes fastest.
Arguments:
- design: bfloat16 [4096, 8192], P('rows', 'cols'), may hold values from -6 to 6
- theta: float32 [8192], P('cols'), may hold values from -0.0625 to 0.0625
- feature_scale: float32 [8192], P('cols'), may hold values from 0.05 to 2
- labels: int32 [4096], P('rows'), may hold values 0 or 1
- psi: bfloat16 [1024, 256], replicated, may hold values from -0.1875 to 0.1875
- phi: float32 [512, 256], replicated, may hold values from -0.25 to 0.25
Outputs:
- newton_step: float32 [8192], P('cols')
- sketch: float32 [256, 8192], P(None, 'cols')
All inputs are finite; a program needn't handle non-finite values. No bound on the sum of `labels` on one device may be relied on, other than what follows from the above.
Results may differ from a plain program's by a relative error of at most 0.0085.
Values sent between devices are 32-bit elements; how exact they have to be, the bound alone decides.
No kernel may reach another device: no remote copies, remote signals or barrier semaphores. Data moves between devices by JAX's collectives and lax.ppermute only.
A program may use at most 128 MiB of HBM per device.

v0:
```python
import jax
import jax.numpy as jnp
from jax import lax
from jax.sharding import PartitionSpec as P

ITERS = 10
damping = 0.01
shrink_share = 0.05
highest = lax.Precision.HIGHEST


def swapped(value, axis, stride):
    mask = 2**stride
    pairs = [(source, source ^ mask) for source in range(lax.axis_size(axis))]
    return lax.ppermute(value, axis, pairs)


def shrink_weights(range_rows):
    width = range_rows.shape[1]
    moment = jnp.dot(range_rows.T, range_rows, precision=highest)
    ridge = shrink_share * jnp.trace(moment) / width
    factor = jnp.linalg.cholesky(moment + ridge * jnp.eye(width, dtype=jnp.float32))
    return jax.scipy.linalg.solve_triangular(factor, range_rows.T, lower=True)


def on_device(design, theta, feature_scale, labels, psi, phi):
    row_devices = lax.axis_size("rows")
    samples = design.shape[0] * row_devices
    width = psi.shape[1]
    scaled_theta = (theta * feature_scale).astype(jnp.bfloat16)
    margins = lax.psum(jnp.dot(design, scaled_theta, preferred_element_type=jnp.float32), "cols")
    chance = jax.nn.sigmoid(margins)
    weight = chance * (1.0 - chance)
    misfit = (chance - labels.astype(jnp.float32)).astype(jnp.bfloat16)
    summed_grad = lax.psum(jnp.dot(misfit, design, preferred_element_type=jnp.float32), "rows")
    gradient = feature_scale * summed_grad / samples + damping * theta
    rows_scaled = (
        design.astype(jnp.float32) * jnp.sqrt(weight)[:, None] * feature_scale[None, :]
    ).astype(jnp.bfloat16)
    mixed_cols = jnp.einsum(
        "rf,rs->fs", rows_scaled, psi, preferred_element_type=jnp.float32
    ).astype(jnp.bfloat16)
    range_rows = lax.psum(
        jnp.dot(rows_scaled, mixed_cols, preferred_element_type=jnp.float32), "cols"
    )
    leaf_weights = shrink_weights(range_rows).astype(jnp.bfloat16)
    sketch = jnp.dot(leaf_weights, rows_scaled, preferred_element_type=jnp.float32)
    position = lax.axis_index("rows")
    for level_bit in range(row_devices.bit_length() - 1):
        partner = swapped(sketch, "rows", level_bit)
        first_low = position // (1 << level_bit) % 2 == 0
        lower_half = jnp.where(first_low, sketch, partner)
        upper_half = jnp.where(first_low, partner, sketch)
        stacked = jnp.concatenate([lower_half, upper_half], 0)
        gram = lax.psum(jnp.dot(stacked, stacked.T, precision=highest), "cols")
        range_rows = jnp.dot(gram, phi, precision=highest)
        sketch = jnp.dot(shrink_weights(range_rows), stacked, precision=highest)
    kernel_part = lax.psum(jnp.dot(sketch, sketch.T, precision=highest), "cols")
    kernel = kernel_part + damping * samples * jnp.eye(width, dtype=jnp.float32)
    kernel_factor = jnp.linalg.cholesky(kernel)
    solution = jnp.zeros_like(gradient)
    residual = gradient

    def precondition_plus(vector):
        projected, squared = lax.psum(
            (jnp.dot(sketch, vector, precision=highest), jnp.sum(vector * vector)), "cols"
        )
        solved = jax.scipy.linalg.cho_solve((kernel_factor, True), projected)
        smoothed = (vector - jnp.dot(solved, sketch, precision=highest)) / damping
        return (smoothed, (squared - jnp.sum(projected * solved)) / damping)

    search, agreement = precondition_plus(residual)
    for turn_index in range(ITERS):
        rounded = (feature_scale * search).astype(jnp.bfloat16)
        forward_rows, length = lax.psum(
            (
                jnp.dot(design, rounded, preferred_element_type=jnp.float32),
                jnp.sum(search * search),
            ),
            "cols",
        )
        inner = (weight * forward_rows).astype(jnp.bfloat16)
        back_sum, bending = lax.psum(
            (
                jnp.dot(inner, design, preferred_element_type=jnp.float32),
                jnp.sum(forward_rows * inner.astype(jnp.float32)),
            ),
            "rows",
        )
        product = feature_scale * back_sum / samples + damping * search
        product, curvature = (product, bending / samples + damping * length)
        step_size = agreement / curvature
        solution = solution + step_size * search
        residual = residual - step_size * product
        if turn_index + 1 < ITERS:
            smoothed, agreement_next = precondition_plus(residual)
            search = smoothed + agreement_next / agreement * search
            agreement = agreement_next
    return (solution, sketch)


def solution(mesh):
    in_specs = (P("rows", "cols"), P("cols"), P("cols"), P("rows"), P(), P())
    out_specs = (P("cols"), P(None, "cols"))
    return jax.shard_map(
        on_device, mesh=mesh, in_specs=in_specs, out_specs=out_specs, check_vma=False
    )
```

profile of v0, /device:TPU:0, one launch (start us, length us, event | category | flops | bytes accessed | tf_op | source)
XLA Modules:
  0.0 1237.9 jit_solution(12997754419069925355)
XLA Ops:
  10.4 23.2 %psum.455 = f32[1024]{0:T(1024)S(1)} all-reduce(f32[1024]{0:T(1024)S(1)} %bitcast.779), channel_id=1, replica_groups=mesh['rows'=4,'cols'=8] {'cols'}, use_global_device_ids=true, to_apply=%region_0.0 | all-reduce | flops 1024 | bytes 8192 | tf_op jit(solution)/shard_map/psum | solution.py:31
  38.1 74.6 %all-reduce.34.cloned.1.call-done = f32[1024,256]{1,0:T(8,128)} async-done(((f32[1024,256]{1,0:T(8,128)}), f32[1024,256]{1,0:T(8,128)}) %all-reduce.34.cloned.1.call-update) | async-done | bytes 1048592 | tf_op jit(solution)/shard_map/psum | solution.py:43
  158.9 19.7 %custom-call.20 = f32[2,128,128]{1,2,0:T(8,128)S(1)} custom-call(f32[2,128,128]{2,1,0:T(8,128)S(1)} %get-tuple-element.28), custom_call_target="InvertDiagBlocksLowerTriangular" | custom-call | tf_op jit(solution)/shard_map/jit(_solve_triangular)/triangular_solve | solution.py:23
  195.7 77.8 %all-reduce.36.cloned.1.call-done = f32[512,512]{1,0:T(8,128)} async-done(((f32[512,512]{1,0:T(8,128)}), f32[512,512]{1,0:T(8,128)}) %all-reduce.36.cloned.1.call-update) | async-done | bytes 1048592 | tf_op jit(solution)/shard_map/psum | solution.py:55
  306.9 12.1 cholesky.265
  328.7 20.5 %custom-call.36 = f32[2,128,128]{1,2,0:T(8,128)S(1)} custom-call(f32[2,128,128]{2,1,0:T(8,128)} %copy-done.15), custom_call_target="InvertDiagBlocksLowerTriangular" | custom-call | tf_op jit(solution)/shard_map/jit(_solve_triangular)/triangular_solve | solution.py:23
  356.2 23.7 %collective-permute-done.1 = f32[256,1024]{1,0:T(8,128)} collective-permute-done((f32[256,1024]{1,0:T(8,128)}, f32[256,1024]{1,0:T(8,128)}, u32[]{:S(2)}, u32[]{:S(2)}) %collective-permute-start.1) | collective-permute-done | bytes 1048608 | tf_op jit(solution)/shard_map/ppermute | solution.py:15
  393.7 71.1 %all-reduce.38.cloned.1.call-done = f32[512,512]{1,0:T(8,128)} async-done(((f32[512,512]{1,0:T(8,128)}), f32[512,512]{1,0:T(8,128)}) %all-reduce.38.cloned.1.call-update) | async-done | bytes 1048592 | tf_op jit(solution)/shard_map/psum | solution.py:55
  498.2 11.9 cholesky.299
  519.8 20.5 %custom-call.38 = f32[2,128,128]{1,2,0:T(8,128)S(1)} custom-call(f32[2,128,128]{2,1,0:T(8,128)} %copy-done.16), custom_call_target="InvertDiagBlocksLowerTriangular" | custom-call | tf_op jit(solution)/shard_map/jit(_solve_triangular)/triangular_solve | solution.py:23
  550.5 20.5 %psum.461 = f32[256]{0:T(256)S(1)} all-reduce(f32[256]{0:T(256)S(1)} %bitcast.781), channel_id=1, replica_groups=mesh['rows'=4,'cols'=8] {'cols'}, use_global_device_ids=true, to_apply=%region_13.16 | all-reduce | flops 256 | bytes 2048 | tf_op jit(solution)/shard_map/psum | solution.py:65
  571.0 47.4 %all-reduce.40.cloned.1.call-done = f32[256,256]{0,1:T(8,128)} async-done(((f32[256,256]{0,1:T(8,128)}), f32[256,256]{0,1:T(8,128)}) %all-reduce.40.cloned.1.call-update) | async-done | bytes 262160 | tf_op jit(solution)/shard_map/psum | solution.py:58
  662.5 19.8 %custom-call.40 = f32[2,128,128]{1,2,0:T(8,128)S(1)} custom-call(f32[2,128,128]{2,1,0:T(8,128)S(1)} %get-tuple-element.91), custom_call_target="InvertDiagBlocksLowerTriangular" | custom-call | tf_op jit(solution)/shard_map/jit(_cho_solve)/triangular_solve | solution.py:68
  686.6 20.6 %all-reduce.19 = (f32[1024]{0:T(1024)S(1)}, f32[]{:T(128)}, f32[]{:T(128)}) all-reduce(f32[1024]{0:T(1024)S(1)} %bitcast.760, f32[]{:T(128)} %get-tuple-element.250, f32[]{:T(128)} %get-tuple-element.248), channel_id=1, replica_groups=mesh['rows'=4,'cols'=8] {'cols'}, use_global_device_ids=true, to_apply=%region_17.21 | all-reduce | flops 1026 | bytes 8208 | tf_op jit(solution)/shard_map/psum | solution.py:75
  720.6 17.8 %all-reduce.18 = (f32[256]{0:T(256)S(1)}, f32[]{:T(128)}) all-reduce(f32[256]{0:T(256)S(1)} %bitcast.792, f32[]{:T(128)} %get-tuple-element.244), channel_id=1, replica_groups=mesh['rows'=4,'cols'=8] {'cols'}, use_global_device_ids=true, to_apply=%region_25.29 | all-reduce | flops 257 | bytes 2056 | tf_op jit(solution)/shard_map/psum | solution.py:65
  744.7 20.0 %all-reduce.17 = (f32[1024]{0:T(1024)S(1)}, f32[]{:T(128)}) all-reduce(f32[1024]{0:T(1024)S(1)} %bitcast.762, f32[]{:T(128)} %get-tuple-element.242), channel_id=1, replica_groups=mesh['rows'=4,'cols'=8] {'cols'}, use_global_device_ids=true, to_apply=%region_27.31 | all-reduce | flops 1025 | bytes 8200 | tf_op jit(solution)/shard_map/psum | solution.py:75
  776.2 17.8 %all-reduce.16 = (f32[256]{0:T(256)S(1)}, f32[]{:T(128)}) all-reduce(f32[256]{0:T(256)S(1)} %bitcast.793, f32[]{:T(128)} %get-tuple-element.238), channel_id=1, replica_groups=mesh['rows'=4,'cols'=8] {'cols'}, use_global_device_ids=true, to_apply=%region_35.39 | all-reduce | flops 257 | bytes 2056 | tf_op jit(solution)/shard_map/psum | solution.py:65
  800.3 20.0 %all-reduce.15 = (f32[1024]{0:T(1024)S(1)}, f32[]{:T(128)}) all-reduce(f32[1024]{0:T(1024)S(1)} %bitcast.764, f32[]{:T(128)} %get-tuple-element.236), channel_id=1, replica_groups=mesh['rows'=4,'cols'=8] {'cols'}, use_global_device_ids=true, to_apply=%region_37.41 | all-reduce | flops 1025 | bytes 8200 | tf_op jit(solution)/shard_map/psum | solution.py:75
  831.8 18.0 %all-reduce.14 = (f32[256]{0:T(256)S(1)}, f32[]{:T(128)}) all-reduce(f32[256]{0:T(256)S(1)} %bitcast.794, f32[]{:T(128)} %get-tuple-element.232), channel_id=1, replica_groups=mesh['rows'=4,'cols'=8] {'cols'}, use_global_device_ids=true, to_apply=%region_45.49 | all-reduce | flops 257 | bytes 2056 | tf_op jit(solution)/shard_map/psum | solution.py:65
  857.7 20.0 %all-reduce.13 = (f32[1024]{0:T(1024)S(1)}, f32[]{:T(128)}) all-reduce(f32[1024]{0:T(1024)S(1)} %bitcast.766, f32[]{:T(128)} %get-tuple-element.230), channel_id=1, replica_groups=mesh['rows'=4,'cols'=8] {'cols'}, use_global_device_ids=true, to_apply=%region_47.51 | all-reduce | flops 1025 | bytes 8200 | tf_op jit(solution)/shard_map/psum | solution.py:75
  889.3 17.8 %all-reduce.12 = (f32[256]{0:T(256)S(1)}, f32[]{:T(128)}) all-reduce(f32[256]{0:T(256)S(1)} %bitcast.795, f32[]{:T(128)} %get-tuple-element.226), channel_id=1, replica_groups=mesh['rows'=4,'cols'=8] {'cols'}, use_global_device_ids=true, to_apply=%region_55.59 | all-reduce | flops 257 | bytes 2056 | tf_op jit(solution)/shard_map/psum | solution.py:65
  915.0 20.0 %all-reduce.11 = (f32[1024]{0:T(1024)S(1)}, f32[]{:T(128)}) all-reduce(f32[1024]{0:T(1024)S(1)} %bitcast.768, f32[]{:T(128)} %get-tuple-element.224), channel_id=1, replica_groups=mesh['rows'=4,'cols'=8] {'cols'}, use_global_device_ids=true, to_apply=%region_57.61 | all-reduce | flops 1025 | bytes 8200 | tf_op jit(solution)/shard_map/psum | solution.py:75
  946.5 17.8 %all-reduce.10 = (f32[256]{0:T(256)S(1)}, f32[]{:T(128)}) all-reduce(f32[256]{0:T(256)S(1)} %bitcast.796, f32[]{:T(128)} %get-tuple-element.220), channel_id=1, replica_groups=mesh['rows'=4,'cols'=8] {'cols'}, use_global_device_ids=true, to_apply=%region_65.69 | all-reduce | flops 257 | bytes 2056 | tf_op jit(solution)/shard_map/psum | solution.py:65
  972.2 20.0 %all-reduce.9 = (f32[1024]{0:T(1024)S(1)}, f32[]{:T(128)}) all-reduce(f32[1024]{0:T(1024)S(1)} %bitcast.770, f32[]{:T(128)} %get-tuple-element.218), channel_id=1, replica_groups=mesh['rows'=4,'cols'=8] {'cols'}, use_global_device_ids=true, to_apply=%region_67.71 | all-reduce | flops 1025 | bytes 8200 | tf_op jit(solution)/shard_map/psum | solution.py:75
  1003.8 17.8 %all-reduce.8 = (f32[256]{0:T(256)S(1)}, f32[]{:T(128)}) all-reduce(f32[256]{0:T(256)S(1)} %bitcast.797, f32[]{:T(128)} %get-tuple-element.214), channel_id=1, replica_groups=mesh['rows'=4,'cols'=8] {'cols'}, use_global_device_ids=true, to_apply=%region_75.79 | all-reduce | flops 257 | bytes 2056 | tf_op jit(solution)/shard_map/psum | solution.py:65
  1029.5 20.0 %all-reduce.7 = (f32[1024]{0:T(1024)S(1)}, f32[]{:T(128)}) all-reduce(f32[1024]{0:T(1024)S(1)} %bitcast.772, f32[]{:T(128)} %get-tuple-element.212), channel_id=1, replica_groups=mesh['rows'=4,'cols'=8] {'cols'}, use_global_device_ids=true, to_apply=%region_77.81 | all-reduce | flops 1025 | bytes 8200 | tf_op jit(solution)/shard_map/psum | solution.py:75
  1061.2 18.0 %all-reduce.6 = (f32[256]{0:T(256)S(1)}, f32[]{:T(128)}) all-reduce(f32[256]{0:T(256)S(1)} %bitcast.798, f32[]{:T(128)} %get-tuple-element.208), channel_id=1, replica_groups=mesh['rows'=4,'cols'=8] {'cols'}, use_global_device_ids=true, to_apply=%region_85.89 | all-reduce | flops 257 | bytes 2056 | tf_op jit(solution)/shard_map/psum | solution.py:65
  1087.1 20.0 %all-reduce.5 = (f32[1024]{0:T(1024)S(1)}, f32[]{:T(128)}) all-reduce(f32[1024]{0:T(1024)S(1)} %bitcast.774, f32[]{:T(128)} %get-tuple-element.206), channel_id=1, replica_groups=mesh['rows'=4,'cols'=8] {'cols'}, use_global_device_ids=true, to_apply=%region_87.91 | all-reduce | flops 1025 | bytes 8200 | tf_op jit(solution)/shard_map/psum | solution.py:75
  1118.8 17.8 %all-reduce.4 = (f32[256]{0:T(256)S(1)}, f32[]{:T(128)}) all-reduce(f32[256]{0:T(256)S(1)} %bitcast.799, f32[]{:T(128)} %get-tuple-element.202), channel_id=1, replica_groups=mesh['rows'=4,'cols'=8] {'cols'}, use_global_device_ids=true, to_apply=%region_95.99 | all-reduce | flops 257 | bytes 2056 | tf_op jit(solution)/shard_map/psum | solution.py:65
  1144.5 20.0 %all-reduce.3 = (f32[1024]{0:T(1024)S(1)}, f32[]{:T(128)}) all-reduce(f32[1024]{0:T(1024)S(1)} %bitcast.776, f32[]{:T(128)} %get-tuple-element.200), channel_id=1, replica_groups=mesh['rows'=4,'cols'=8] {'cols'}, use_global_device_ids=true, to_apply=%region_97.101 | all-reduce | flops 1025 | bytes 8200 | tf_op jit(solution)/shard_map/psum | solution.py:75
  1176.1 17.8 %all-reduce.2 = (f32[256]{0:T(256)S(1)}, f32[]{:T(128)}) all-reduce(f32[256]{0:T(256)S(1)} %bitcast.800, f32[]{:T(128)} %get-tuple-element.196), channel_id=1, replica_groups=mesh['rows'=4,'cols'=8] {'cols'}, use_global_device_ids=true, to_apply=%region_105.109 | all-reduce | flops 257 | bytes 2056 | tf_op jit(solution)/shard_map/psum | solution.py:65
  1201.9 20.0 %all-reduce.1 = (f32[1024]{0:T(1024)S(1)}, f32[]{:T(128)}) all-reduce(f32[1024]{0:T(1024)S(1)} %bitcast.778, f32[]{:T(128)} %get-tuple-element.194), channel_id=1, replica_groups=mesh['rows'=4,'cols'=8] {'cols'}, use_global_device_ids=true, to_apply=%region_107.111 | all-reduce | flops 1025 | bytes 8200 | tf_op jit(solution)/shard_map/psum | solution.py:75
  (370 shorter events, 406.0 us)
Async XLA Ops:
  7.2 26.4 %copy-start = (bf16[1024,256]{1,0:T(8,128)(2,1)S(1)}, bf16[1024,256]{1,0:T(8,128)(2,1)}, u32[]{:S(2)}) copy-start(bf16[1024,256]{1,0:T(8,128)(2,1)} %param.15) | copy-start | bytes 1572868
  7.2 26.4 %copy-start.10 = (f32[1024]{0:T(1024)S(1)}, f32[1024]{0:T(1024)}, u32[]{:S(2)}) copy-start(f32[1024]{0:T(1024)} %param.13) | copy-start | bytes 12292
  7.2 26.4 %copy-start.1 = (bf16[1024,1024]{1,0:T(8,128)(2,1)S(1)}, bf16[1024,1024]{1,0:T(8,128)(2,1)}, u32[]{:S(2)}) copy-start(bf16[1024,1024]{1,0:T(8,128)(2,1)} %param.11) | copy-start | bytes 6291460
  7.2 26.3 %copy-start.18 = (s32[1024]{0:T(1024)S(1)}, s32[1024]{0:T(1024)}, u32[]{:S(2)}) copy-start(s32[1024]{0:T(1024)} %param.14) | copy-start | bytes 12292
  7.2 105.5 %all-reduce.34.cloned.1.call-start = ((), (), s32[]{:S(2)}) async-start(), calls=%async_computation | async-start | bytes 2097152 | tf_op jit(solution)/shard_map/psum | solution.py:43
  36.9 236.6 %all-reduce.36.cloned.1.call-start = ((), (), s32[]{:S(2)}) async-start(), calls=%async_computation.1 | async-start | bytes 2097152 | tf_op jit(solution)/shard_map/psum | solution.py:55
  158.9 19.7 %copy-start.19 = (s32[2,2]{1,0:T(2,128)}, s32[2,2]{1,0:T(2,128)S(1)}, u32[]{:S(2)}) copy-start(s32[2,2]{1,0:T(2,128)S(1)} %get-tuple-element.492) | copy-start | bytes 52
  184.8 3.0 collective-permute-start
  189.5 1.0 copy-start.7
  189.5 1.3 copy-start.9
  195.4 269.4 %all-reduce.38.cloned.1.call-start = ((), (), s32[]{:S(2)}) async-start(), calls=%async_computation.2 | async-start | bytes 2097152 | tf_op jit(solution)/shard_map/psum | solution.py:55
  281.8 0.7 copy-start.13
  319.0 2.6 copy-start.11
  328.0 0.6 copy-start.15
  349.2 1.5 copy-start.8
  354.7 25.2 %collective-permute-start.1 = (f32[256,1024]{1,0:T(8,128)}, f32[256,1024]{1,0:T(8,128)}, u32[]{:S(2)}, u32[]{:S(2)}) collective-permute-start(f32[256,1024]{1,0:T(8,128)} %fusion.2), channel_id=1, source_target_pairs={{0,16},{8,24},{16,0},{24,8},{1,17},{9,25},{17,1},{25,9},{2,18},{10... | collective-permute-start | bytes 3145736 | tf_op jit(solution)/shard_map/ppermute | solution.py:15
  381.6 1.0 copy-start.4
  381.6 1.3 copy-start.6
  387.5 231.0 %all-reduce.40.cloned.1.call-start = ((), (), s32[]{:S(2)}) async-start(), calls=%async_computation.3 | async-start | bytes 524288 | tf_op jit(solution)/shard_map/psum | solution.py:58
  473.1 0.7 copy-start.14
  510.1 2.6 copy-start.12
  519.2 0.6 copy-start.16
  540.3 1.5 copy-start.5
  544.9 1.0 copy-start.2
  545.9 1.8 copy-start.17
  662.5 132.3 %copy-start.3 = (f32[256,256]{1,0:T(8,128)}, f32[256,256]{1,0:T(8,128)S(1)}, u32[]{:S(2)}) copy-start(f32[256,256]{1,0:T(8,128)S(1)} %get-tuple-element.476) | copy-start | bytes 786436
Sparse Core Ops, SparseCore 0:
  37.0 75.6 all-reduce.33
  195.5 77.9 all-reduce.35
  387.6 77.2 all-reduce.37
  547.8 70.6 all-reduce.39
where the time goes:
time: 1240 us
  blocking collectives  475 us (38%)
  waiting for transfers between devices  298 us (24%)
  other arithmetic  259 us (21%)
  matrix products  123 us (10%)
  between operations  48.4 us (4%)
  local copies, waits for them, and re-layouts  32 us (3%)
    psum x10, blocking collectives, on_device(): lax.psum((jnp.dot(design, rounded, preferred_element_type=jnp.float32), j...  201 us
    psum x10, blocking collectives, precondition_plus(): lax.psum((jnp.dot(sketch, vector, precision=highest), jnp.sum(vector * ve...  181 us
    psum x2, waiting for transfers between devices, on_device(): gram = lax.psum(jnp.dot(stacked, stacked.T, precision=highest), 'cols')  149 us
    another operation x20, other arithmetic, shrink_weights(): jnp.linalg.cholesky(moment + ridge * jnp.eye(width, dtype=jnp.float32))  105 us
    psum x1, waiting for transfers between devices, on_device(): lax.psum(jnp.dot(rows_scaled, mixed_cols, preferred_element_type=jnp.floa...  74.6 us
    psum x10, blocking collectives, on_device(): lax.psum((jnp.dot(inner, design, preferred_element_type=jnp.float32), jnp...  64.5 us
    another operation x7, other arithmetic, shrink_weights(): return jax.scipy.linalg.solve_triangular(factor, range_rows.T, lower=True)  63.2 us
    psum x1, waiting for transfers between devices, on_device(): kernel_part = lax.psum(jnp.dot(sketch, sketch.T, precision=highest), 'cols')  47.4 us
  transfers between devices with their start and end apart: 6, of which 6 were waited for; matrix products, arithmetic and copies ran while one was open for 0% of the time, Pallas kernels for 0%

commit v1 on v0

--- a/solution.py
+++ b/solution.py
@@ -52,7 +52,9 @@
         lower_half = jnp.where(first_low, sketch, partner)
         upper_half = jnp.where(first_low, partner, sketch)
         stacked = jnp.concatenate([lower_half, upper_half], 0)
-        gram = lax.psum(jnp.dot(stacked, stacked.T, precision=highest), "cols")
+        gram = jnp.sum(
+            lax.all_gather(jnp.dot(stacked, stacked.T, precision=highest), "cols"), axis=0
+        )
         range_rows = jnp.dot(gram, phi, precision=highest)
         sketch = jnp.dot(shrink_weights(range_rows), stacked, precision=highest)
     kernel_part = lax.psum(jnp.dot(sketch, sketch.T, precision=highest), "cols")

time: 1240 us -> 1350 us (1.089)
  waiting for transfers between devices: 298 us -> 390 us
    all_gather x0 -> x2, waiting for transfers between devices: none -> 241 us  [on_device(): lax.all_gather(jnp.dot(stacked, stacked.T, precision=highest), 'cols')]
    psum x2 -> x0, waiting for transfers between devices: 149 us -> none  [on_device(): gram = lax.psum(jnp.dot(stacked, stacked.T, precision=highest), 'cols')]
where the time goes in v1:
time: 1350 us; the launch traced here: 1340 us
  blocking collectives  473 us (35%)
  waiting for transfers between devices  390 us (29%)
  other arithmetic  270 us (20%)
  matrix products  123 us (9%)
  between operations  48.4 us (4%)
  local copies, waits for them, and re-layouts  32 us (2%)
    all_gather x2, waiting for transfers between devices, on_device(): lax.all_gather(jnp.dot(stacked, stacked.T, precision=highest), 'cols')  241 us
    psum x10, blocking collectives, on_device(): lax.psum((jnp.dot(design, rounded, preferred_element_type=jnp.float32), j...  201 us
    psum x10, blocking collectives, precondition_plus(): lax.psum((jnp.dot(sketch, vector, precision=highest), jnp.sum(vector * ve...  179 us
    another operation x20, other arithmetic, shrink_weights(): jnp.linalg.cholesky(moment + ridge * jnp.eye(width, dtype=jnp.float32))  105 us
    psum x1, waiting for transfers between devices, on_device(): lax.psum(jnp.dot(rows_scaled, mixed_cols, preferred_element_type=jnp.floa...  74.6 us
    psum x10, blocking collectives, on_device(): lax.psum((jnp.dot(inner, design, preferred_element_type=jnp.float32), jnp...  64.5 us
    another operation x7, other arithmetic, shrink_weights(): return jax.scipy.linalg.solve_triangular(factor, range_rows.T, lower=True)  63.2 us
    psum x1, waiting for transfers between devices, on_device(): kernel_part = lax.psum(jnp.dot(sketch, sketch.T, precision=highest), 'cols')  47.7 us
  transfers between devices with their start and end apart: 6, of which 6 were waited for; matrix products, arithmetic and copies ran while one was open for 0% of the time, Pallas kernels for 0%

profile of v1, /device:TPU:0, one launch (start us, length us, event | category | flops | bytes accessed | tf_op | source)
XLA Modules:
  0.0 1339.1 jit_solution(1096300679722532463)
XLA Ops:
  10.4 23.2 %psum.441 = f32[1024]{0:T(1024)S(1)} all-reduce(f32[1024]{0:T(1024)S(1)} %bitcast.783), channel_id=1, replica_groups=mesh['rows'=4,'cols'=8] {'cols'}, use_global_device_ids=true, to_apply=%region_0.0 | all-reduce | flops 1024 | bytes 8192 | tf_op jit(solution)/shard_map/psum | solution.py:31
  38.1 74.6 %all-reduce.32.cloned.1.call-done = f32[1024,256]{1,0:T(8,128)} async-done(((f32[1024,256]{1,0:T(8,128)}), f32[1024,256]{1,0:T(8,128)}) %all-reduce.32.cloned.1.call-update) | async-done | bytes 1048592 | tf_op jit(solution)/shard_map/psum | solution.py:43
  158.9 19.7 %custom-call.20 = f32[2,128,128]{1,2,0:T(8,128)S(1)} custom-call(f32[2,128,128]{2,1,0:T(8,128)S(1)} %get-tuple-element.28), custom_call_target="InvertDiagBlocksLowerTriangular" | custom-call | tf_op jit(solution)/shard_map/jit(_solve_triangular)/triangular_solve | solution.py:23
  195.7 124.0 %all-gather.5.cloned.1.call-done = f32[4096,512]{1,0:T(8,128)} async-done(((f32[512,512]{1,0:T(8,128)}), f32[4096,512]{1,0:T(8,128)}) %all-gather.5.cloned.1.call-update) | async-done | bytes 8388624 | tf_op jit(solution)/shard_map/all_gather | solution.py:56
  358.3 12.1 cholesky.265
  380.3 20.5 %custom-call.36 = f32[2,128,128]{1,2,0:T(8,128)S(1)} custom-call(f32[2,128,128]{2,1,0:T(8,128)} %copy-done.15), custom_call_target="InvertDiagBlocksLowerTriangular" | custom-call | tf_op jit(solution)/shard_map/jit(_solve_triangular)/triangular_solve | solution.py:23
  407.8 23.0 %collective-permute-done.1 = f32[256,1024]{1,0:T(8,128)} collective-permute-done((f32[256,1024]{1,0:T(8,128)}, f32[256,1024]{1,0:T(8,128)}, u32[]{:S(2)}, u32[]{:S(2)}) %collective-permute-start.1) | collective-permute-done | bytes 1048608 | tf_op jit(solution)/shard_map/ppermute | solution.py:15
  444.7 117.3 %all-gather.7.cloned.1.call-done = f32[4096,512]{1,0:T(8,128)} async-done(((f32[512,512]{1,0:T(8,128)}), f32[4096,512]{1,0:T(8,128)}) %all-gather.7.cloned.1.call-update) | async-done | bytes 8388624 | tf_op jit(solution)/shard_map/all_gather | solution.py:56
  600.6 11.9 cholesky.299
  622.4 20.5 %custom-call.38 = f32[2,128,128]{1,2,0:T(8,128)S(1)} custom-call(f32[2,128,128]{2,1,0:T(8,128)} %copy-done.16), custom_call_target="InvertDiagBlocksLowerTriangular" | custom-call | tf_op jit(solution)/shard_map/jit(_solve_triangular)/triangular_solve | solution.py:23
  653.0 18.9 %psum.445 = f32[256]{0:T(256)S(1)} all-reduce(f32[256]{0:T(256)S(1)} %bitcast.785), channel_id=1, replica_groups=mesh['rows'=4,'cols'=8] {'cols'}, use_global_device_ids=true, to_apply=%region_13.16 | all-reduce | flops 256 | bytes 2048 | tf_op jit(solution)/shard_map/psum | solution.py:67
  672.0 47.7 %all-reduce.34.cloned.1.call-done = f32[256,256]{0,1:T(8,128)} async-done(((f32[256,256]{0,1:T(8,128)}), f32[256,256]{0,1:T(8,128)}) %all-reduce.34.cloned.1.call-update) | async-done | bytes 262160 | tf_op jit(solution)/shard_map/psum | solution.py:60
  763.7 19.8 %custom-call.40 = f32[2,128,128]{1,2,0:T(8,128)S(1)} custom-call(f32[2,128,128]{2,1,0:T(8,128)S(1)} %get-tuple-element.91), custom_call_target="InvertDiagBlocksLowerTriangular" | custom-call | tf_op jit(solution)/shard_map/jit(_cho_solve)/triangular_solve | solution.py:70
  787.8 20.6 %all-reduce.19 = (f32[1024]{0:T(1024)S(1)}, f32[]{:T(128)}, f32[]{:T(128)}) all-reduce(f32[1024]{0:T(1024)S(1)} %bitcast.764, f32[]{:T(128)} %get-tuple-element.250, f32[]{:T(128)} %get-tuple-element.248), channel_id=1, replica_groups=mesh['rows'=4,'cols'=8] {'cols'}, use_global_device_ids=true, to_apply=%region_17.21 | all-reduce | flops 1026 | bytes 8208 | tf_op jit(solution)/shard_map/psum | solution.py:77
  821.9 17.8 %all-reduce.18 = (f32[256]{0:T(256)S(1)}, f32[]{:T(128)}) all-reduce(f32[256]{0:T(256)S(1)} %bitcast.796, f32[]{:T(128)} %get-tuple-element.244), channel_id=1, replica_groups=mesh['rows'=4,'cols'=8] {'cols'}, use_global_device_ids=true, to_apply=%region_25.29 | all-reduce | flops 257 | bytes 2056 | tf_op jit(solution)/shard_map/psum | solution.py:67
  845.9 20.0 %all-reduce.17 = (f32[1024]{0:T(1024)S(1)}, f32[]{:T(128)}) all-reduce(f32[1024]{0:T(1024)S(1)} %bitcast.766, f32[]{:T(128)} %get-tuple-element.242), channel_id=1, replica_groups=mesh['rows'=4,'cols'=8] {'cols'}, use_global_device_ids=true, to_apply=%region_27.31 | all-reduce | flops 1025 | bytes 8200 | tf_op jit(solution)/shard_map/psum | solution.py:77
  877.4 17.8 %all-reduce.16 = (f32[256]{0:T(256)S(1)}, f32[]{:T(128)}) all-reduce(f32[256]{0:T(256)S(1)} %bitcast.797, f32[]{:T(128)} %get-tuple-element.238), channel_id=1, replica_groups=mesh['rows'=4,'cols'=8] {'cols'}, use_global_device_ids=true, to_apply=%region_35.39 | all-reduce | flops 257 | bytes 2056 | tf_op jit(solution)/shard_map/psum | solution.py:67
  901.5 20.0 %all-reduce.15 = (f32[1024]{0:T(1024)S(1)}, f32[]{:T(128)}) all-reduce(f32[1024]{0:T(1024)S(1)} %bitcast.768, f32[]{:T(128)} %get-tuple-element.236), channel_id=1, replica_groups=mesh['rows'=4,'cols'=8] {'cols'}, use_global_device_ids=true, to_apply=%region_37.41 | all-reduce | flops 1025 | bytes 8200 | tf_op jit(solution)/shard_map/psum | solution.py:77
  933.0 18.0 %all-reduce.14 = (f32[256]{0:T(256)S(1)}, f32[]{:T(128)}) all-reduce(f32[256]{0:T(256)S(1)} %bitcast.798, f32[]{:T(128)} %get-tuple-element.232), channel_id=1, replica_groups=mesh['rows'=4,'cols'=8] {'cols'}, use_global_device_ids=true, to_apply=%region_45.49 | all-reduce | flops 257 | bytes 2056 | tf_op jit(solution)/shard_map/psum | solution.py:67
  959.0 20.0 %all-reduce.13 = (f32[1024]{0:T(1024)S(1)}, f32[]{:T(128)}) all-reduce(f32[1024]{0:T(1024)S(1)} %bitcast.770, f32[]{:T(128)} %get-tuple-element.230), channel_id=1, replica_groups=mesh['rows'=4,'cols'=8] {'cols'}, use_global_device_ids=true, to_apply=%region_47.51 | all-reduce | flops 1025 | bytes 8200 | tf_op jit(solution)/shard_map/psum | solution.py:77
  990.5 17.8 %all-reduce.12 = (f32[256]{0:T(256)S(1)}, f32[]{:T(128)}) all-reduce(f32[256]{0:T(256)S(1)} %bitcast.799, f32[]{:T(128)} %get-tuple-element.226), channel_id=1, replica_groups=mesh['rows'=4,'cols'=8] {'cols'}, use_global_device_ids=true, to_apply=%region_55.59 | all-reduce | flops 257 | bytes 2056 | tf_op jit(solution)/shard_map/psum | solution.py:67
  1016.2 20.0 %all-reduce.11 = (f32[1024]{0:T(1024)S(1)}, f32[]{:T(128)}) all-reduce(f32[1024]{0:T(1024)S(1)} %bitcast.772, f32[]{:T(128)} %get-tuple-element.224), channel_id=1, replica_groups=mesh['rows'=4,'cols'=8] {'cols'}, use_global_device_ids=true, to_apply=%region_57.61 | all-reduce | flops 1025 | bytes 8200 | tf_op jit(solution)/shard_map/psum | solution.py:77
  1047.7 17.8 %all-reduce.10 = (f32[256]{0:T(256)S(1)}, f32[]{:T(128)}) all-reduce(f32[256]{0:T(256)S(1)} %bitcast.800, f32[]{:T(128)} %get-tuple-element.220), channel_id=1, replica_groups=mesh['rows'=4,'cols'=8] {'cols'}, use_global_device_ids=true, to_apply=%region_65.69 | all-reduce | flops 257 | bytes 2056 | tf_op jit(solution)/shard_map/psum | solution.py:67
  1073.4 20.0 %all-reduce.9 = (f32[1024]{0:T(1024)S(1)}, f32[]{:T(128)}) all-reduce(f32[1024]{0:T(1024)S(1)} %bitcast.774, f32[]{:T(128)} %get-tuple-element.218), channel_id=1, replica_groups=mesh['rows'=4,'cols'=8] {'cols'}, use_global_device_ids=true, to_apply=%region_67.71 | all-reduce | flops 1025 | bytes 8200 | tf_op jit(solution)/shard_map/psum | solution.py:77
  1105.0 17.8 %all-reduce.8 = (f32[256]{0:T(256)S(1)}, f32[]{:T(128)}) all-reduce(f32[256]{0:T(256)S(1)} %bitcast.801, f32[]{:T(128)} %get-tuple-element.214), channel_id=1, replica_groups=mesh['rows'=4,'cols'=8] {'cols'}, use_global_device_ids=true, to_apply=%region_75.79 | all-reduce | flops 257 | bytes 2056 | tf_op jit(solution)/shard_map/psum | solution.py:67
  1130.7 20.0 %all-reduce.7 = (f32[1024]{0:T(1024)S(1)}, f32[]{:T(128)}) all-reduce(f32[1024]{0:T(1024)S(1)} %bitcast.776, f32[]{:T(128)} %get-tuple-element.212), channel_id=1, replica_groups=mesh['rows'=4,'cols'=8] {'cols'}, use_global_device_ids=true, to_apply=%region_77.81 | all-reduce | flops 1025 | bytes 8200 | tf_op jit(solution)/shard_map/psum | solution.py:77
  1162.4 18.0 %all-reduce.6 = (f32[256]{0:T(256)S(1)}, f32[]{:T(128)}) all-reduce(f32[256]{0:T(256)S(1)} %bitcast.802, f32[]{:T(128)} %get-tuple-element.208), channel_id=1, replica_groups=mesh['rows'=4,'cols'=8] {'cols'}, use_global_device_ids=true, to_apply=%region_85.89 | all-reduce | flops 257 | bytes 2056 | tf_op jit(solution)/shard_map/psum | solution.py:67
  1188.3 20.0 %all-reduce.5 = (f32[1024]{0:T(1024)S(1)}, f32[]{:T(128)}) all-reduce(f32[1024]{0:T(1024)S(1)} %bitcast.778, f32[]{:T(128)} %get-tuple-element.206), channel_id=1, replica_groups=mesh['rows'=4,'cols'=8] {'cols'}, use_global_device_ids=true, to_apply=%region_87.91 | all-reduce | flops 1025 | bytes 8200 | tf_op jit(solution)/shard_map/psum | solution.py:77
  1220.0 17.8 %all-reduce.4 = (f32[256]{0:T(256)S(1)}, f32[]{:T(128)}) all-reduce(f32[256]{0:T(256)S(1)} %bitcast.803, f32[]{:T(128)} %get-tuple-element.202), channel_id=1, replica_groups=mesh['rows'=4,'cols'=8] {'cols'}, use_global_device_ids=true, to_apply=%region_95.99 | all-reduce | flops 257 | bytes 2056 | tf_op jit(solution)/shard_map/psum | solution.py:67
  1245.7 20.0 %all-reduce.3 = (f32[1024]{0:T(1024)S(1)}, f32[]{:T(128)}) all-reduce(f32[1024]{0:T(1024)S(1)} %bitcast.780, f32[]{:T(128)} %get-tuple-element.200), channel_id=1, replica_groups=mesh['rows'=4,'cols'=8] {'cols'}, use_global_device_ids=true, to_apply=%region_97.101 | all-reduce | flops 1025 | bytes 8200 | tf_op jit(solution)/shard_map/psum | solution.py:77
  1277.3 17.8 %all-reduce.2 = (f32[256]{0:T(256)S(1)}, f32[]{:T(128)}) all-reduce(f32[256]{0:T(256)S(1)} %bitcast.804, f32[]{:T(128)} %get-tuple-element.196), channel_id=1, replica_groups=mesh['rows'=4,'cols'=8] {'cols'}, use_global_device_ids=true, to_apply=%region_105.109 | all-reduce | flops 257 | bytes 2056 | tf_op jit(solution)/shard_map/psum | solution.py:67
  1303.1 20.0 %all-reduce.1 = (f32[1024]{0:T(1024)S(1)}, f32[]{:T(128)}) all-reduce(f32[1024]{0:T(1024)S(1)} %bitcast.782, f32[]{:T(128)} %get-tuple-element.194), channel_id=1, replica_groups=mesh['rows'=4,'cols'=8] {'cols'}, use_global_device_ids=true, to_apply=%region_107.111 | all-reduce | flops 1025 | bytes 8200 | tf_op jit(solution)/shard_map/psum | solution.py:77
  (372 shorter events, 417.1 us)
Async XLA Ops:
  7.2 26.4 %copy-start = (bf16[1024,256]{1,0:T(8,128)(2,1)S(1)}, bf16[1024,256]{1,0:T(8,128)(2,1)}, u32[]{:S(2)}) copy-start(bf16[1024,256]{1,0:T(8,128)(2,1)} %param.15) | copy-start | bytes 1572868
  7.2 26.4 %copy-start.10 = (f32[1024]{0:T(1024)S(1)}, f32[1024]{0:T(1024)}, u32[]{:S(2)}) copy-start(f32[1024]{0:T(1024)} %param.13) | copy-start | bytes 12292
  7.2 26.4 %copy-start.1 = (bf16[1024,1024]{1,0:T(8,128)(2,1)S(1)}, bf16[1024,1024]{1,0:T(8,128)(2,1)}, u32[]{:S(2)}) copy-start(bf16[1024,1024]{1,0:T(8,128)(2,1)} %param.11) | copy-start | bytes 6291460
  7.2 26.3 %copy-start.18 = (s32[1024]{0:T(1024)S(1)}, s32[1024]{0:T(1024)}, u32[]{:S(2)}) copy-start(s32[1024]{0:T(1024)} %param.14) | copy-start | bytes 12292
  7.2 105.5 %all-reduce.32.cloned.1.call-start = ((), (), s32[]{:S(2)}) async-start(), calls=%async_computation | async-start | bytes 2097152 | tf_op jit(solution)/shard_map/psum | solution.py:43
  36.9 282.7 %all-gather.5.cloned.1.call-start = ((), (), s32[]{:S(2)}) async-start(), calls=%async_computation.2 | async-start | bytes 9437184 | tf_op jit(solution)/shard_map/all_gather | solution.py:56
  158.9 19.7 %copy-start.19 = (s32[2,2]{1,0:T(2,128)}, s32[2,2]{1,0:T(2,128)S(1)}, u32[]{:S(2)}) copy-start(s32[2,2]{1,0:T(2,128)S(1)} %get-tuple-element.492) | copy-start | bytes 52
  184.8 3.0 collective-permute-start
  189.5 1.1 copy-start.7
  189.5 1.3 copy-start.9
  195.4 366.5 %all-gather.7.cloned.1.call-start = ((), (), s32[]{:S(2)}) async-start(), calls=%async_computation.3 | async-start | bytes 9437184 | tf_op jit(solution)/shard_map/all_gather | solution.py:56
  333.2 0.7 copy-start.13
  370.4 2.7 copy-start.11
  379.6 0.6 copy-start.15
  400.8 1.5 copy-start.8
  406.3 24.5 %collective-permute-start.1 = (f32[256,1024]{1,0:T(8,128)}, f32[256,1024]{1,0:T(8,128)}, u32[]{:S(2)}, u32[]{:S(2)}) collective-permute-start(f32[256,1024]{1,0:T(8,128)} %fusion.2), channel_id=1, source_target_pairs={{0,16},{8,24},{16,0},{24,8},{1,17},{9,25},{17,1},{25,9},{2,18},{10... | collective-permute-start | bytes 3145736 | tf_op jit(solution)/shard_map/ppermute | solution.py:15
  432.6 1.1 copy-start.4
  432.6 1.3 copy-start.6
  438.4 281.2 %all-reduce.34.cloned.1.call-start = ((), (), s32[]{:S(2)}) async-start(), calls=%async_computation.1 | async-start | bytes 524288 | tf_op jit(solution)/shard_map/psum | solution.py:60
  575.5 0.7 copy-start.14
  612.5 2.7 copy-start.12
  621.7 0.6 copy-start.16
  642.9 1.5 copy-start.5
  647.5 1.0 copy-start.2
  648.4 1.8 copy-start.17
  763.7 132.3 %copy-start.3 = (f32[256,256]{1,0:T(8,128)}, f32[256,256]{1,0:T(8,128)S(1)}, u32[]{:S(2)}) copy-start(f32[256,256]{1,0:T(8,128)S(1)} %get-tuple-element.476) | copy-start | bytes 786436
Sparse Core Ops, SparseCore 0:
  37.0 75.6 all-reduce.31
  195.5 124.0 all-gather.4
  438.5 123.3 all-gather.6
  650.3 69.2 all-reduce.33
